TPU v7x, 32 devices: a whole 2x2x4 slice. The times are simulated.
32 devices in a mesh: ta: 16 (over z, y, x), sa: 2 (over core).
Axes of the slice: x: 2, y: 2, z: 4, core: 2. Of those that a mesh axis runs over, the one named last changes fastest.
Arguments:
- rhs: float32 [1, 2, 40, 16, 2, 128], P(None, None, None, 'ta', 'sa'), may hold values from -6 to 6
- links: bfloat16 [4, 2, 40, 40, 16, 2, 128], P(None, None, None, None, 'ta', 'sa'), may hold values from -0.625 to 0.625
- clover: bfloat16 [2, 40, 40, 16, 2, 128], P(None, None, None, 'ta', 'sa'), may hold values from -1 to 7
- mr_steps: int32 [16, 2, 2], P('ta', 'sa'), may hold values from 2 to 3
Outputs:
- solution: float32 [1, 2, 40, 16, 2, 128], P(None, None, None, 'ta', 'sa')
- residual: float32 [1, 2, 40, 16, 2, 128], P(None, None, None, 'ta', 'sa')
All inputs are finite; a program needn't handle non-finite values.
Results may differ from a plain program's by a relative error of at most 0.0003.
Values sent between devices are 32-bit elements; how exact they have to be, the bound alone decides.
A program may use at most 128 MiB of HBM per device.

v0:
```python
import functools

import jax
import jax.numpy as jnp
from jax import lax
from jax.experimental import pallas as pl
from jax.experimental.pallas import tpu as pltpu
from jax.sharding import PartitionSpec as P

LZ = 4
LY = 4
LX = 4
MR_MAX = 3
SWEEPS = 2
PHASES = 2 * SWEEPS
UNROLL = 10
PREPARE_UNROLL = 8
MESH = pl.DeviceIdType.MESH


def kernel(
    nt,
    nz,
    rhs_hbm,
    links_ref,
    clover_ref,
    steps_hbm,
    x_ref,
    r_ref,
    rhs_ref,
    steps_ref,
    lk,
    cl,
    g,
    rs,
    xs,
    s_ref,
    e_ref,
    acc,
    a_ref,
    gv,
    f_ref,
    sbuf,
    rbuf,
    csem,
    ssem,
    rsem,
):
    dof, lanes = rhs_ref.shape[1:]
    half = lanes // 2
    tiles = dof // 8
    ta = lax.axis_index("ta")
    sa = lax.axis_index("sa")
    t_next, t_prev = lax.rem(ta + 1, nt), lax.rem(ta + nt - 1, nt)
    z_next, z_prev = lax.rem(sa + 1, nz), lax.rem(sa + nz - 1, nz)

    copies = [
        pltpu.make_async_copy(links_ref.at[d], lk.at[d], csem.at[d]) for d in range(4)
    ] + [
        pltpu.make_async_copy(clover_ref, cl, csem.at[4]),
        pltpu.make_async_copy(rhs_hbm, rhs_ref, csem.at[5]),
        pltpu.make_async_copy(steps_hbm, steps_ref, csem.at[6]),
    ]
    for d in (5, 1, 2, 0, 3, 4, 6):
        copies[d].start()

    barrier = pltpu.get_barrier_semaphore()
    for where_to in ({"ta": t_next}, {"ta": t_prev}, {"sa": z_next}, {"sa": z_prev}):
        pl.semaphore_signal(barrier, inc=1, device_id=where_to, device_id_type=MESH)

    shape = (dof, lanes)
    lane = lax.broadcasted_iota(jnp.int32, shape, 1)
    row = lax.broadcasted_iota(jnp.int32, shape, 0)
    signs = jnp.where(row < dof // 2, 1.0, -1.0).astype(jnp.float32)
    low = lane < half
    site = lane % half
    zpos = site // (LY * LX)
    ypos = site // LX % LY
    xpos = site % LX
    z_last, z_first = zpos == LZ - 1, zpos == 0
    y_last, y_first = ypos == LY - 1, ypos == 0
    x_last, x_first = xpos == LX - 1, xpos == 0
    zero = jnp.zeros(shape, jnp.float32)
    plane = LY * LX

    def roll(v, by):
        return pltpu.roll(v, by % lanes, 1)

    copies[5].wait()
    for c in range(2):
        v = rhs_ref[c]
        w = roll(v, half)
        rs[0, c] = jnp.where(low, v, w)
        rs[1, c] = jnp.where(low, w, v)
        xs[0, c] = zero
        xs[1, c] = zero

    def prepare(plain, rolled, groups):
        def body(outer, carry):
            for inner in range(PREPARE_UNROLL):
                i = outer * PREPARE_UNROLL + inner
                for c in range(2):
                    b = roll(rolled(c, i).astype(jnp.float32), half)
                    for source, group in zip(plain, groups):
                        a = source(c, i).astype(jnp.float32)
                        g[group, 0, c, i] = jnp.where(low, a, b)
                        g[group, 1, c, i] = jnp.where(low, b, a)
            return carry

        lax.fori_loop(0, dof // PREPARE_UNROLL, body, 0)

    def link(d):
        return lambda c, i: lk[d, c, i]

    for d in (1, 2, 0):
        copies[d].wait()
    prepare([link(2), link(0)], link(1), [0, 3])
    for d in (3, 4, 6):
        copies[d].wait()
    prepare([lambda c, i: cl[c, i], link(0)], link(3), [1, 2])

    def fold(v):
        total = v[0:8]
        for t in range(1, tiles):
            total = total + v[8 * t : 8 * t + 8]
        return total

    def gathered(slot):
        parts = []
        for t in range(tiles):
            total = None
            for k in range(8):
                piece = f_ref[slot, pl.ds(8 * 8 * t + k, 8, stride=8), :]
                total = piece if total is None else total + piece
            parts.append(total)
        return jnp.concatenate(parts, axis=0)

    def sweep_matrices(forward, forward_half, inputs, backward, backward_half, more):
        vr, vi = inputs
        vs = vr + vi
        shared = backward == forward

        def one(i, carry):
            mr, mi = g[forward, forward_half, 0, i], g[forward, forward_half, 1, i]
            ms = mr + mi
            p1 = fold(mr * vr)
            p2 = fold(mi * vi)
            p3 = fold(ms * vs)
            at = pl.multiple_of(8 * i, 8)
            real_part, imag_part = p1 - p2, p3 - p1 - p2
            if more:
                real_part = real_part + f_ref[0, pl.ds(at, 8), :]
                imag_part = imag_part + f_ref[1, pl.ds(at, 8), :]
            f_ref[0, pl.ds(at, 8), :] = real_part
            f_ref[1, pl.ds(at, 8), :] = imag_part
            if backward is None:
                return carry
            if not shared:
                mr, mi = g[backward, backward_half, 0, i], g[backward, backward_half, 1, i]
                ms = mr + mi
            b1, b2, b3 = carry
            br = gv[0, pl.ds(i, 1), :]
            bi = gv[1, pl.ds(i, 1), :]
            bd = gv[2, pl.ds(i, 1), :]
            return (b1 + mr * br, b2 + mi * bi, b3 + ms * bd)

        def body(outer, carry):
            for inner in range(UNROLL):
                carry = one(outer * UNROLL + inner, carry)
            return carry

        start = 0 if backward is None else (zero, zero, zero)
        got = lax.fori_loop(0, dof // UNROLL, body, start)
        if backward is None:
            return None
        b1, b2, b3 = got
        return -signs * (b1 + b2), -signs * (b1 - b2 - b3)

    def phase(ph, token):
        h = lax.rem(ph + sa, 2)
        other = 1 - h
        limit = steps_ref[h]
        first = (lane // half) == h
        h_is_0 = (lane * 0 + h) == 0

        def ahead(v):
            n = -v
            ya = jnp.where(y_last, roll(n, (LY - 1) * LX), roll(n, -LX))
            za = jnp.where(z_last, 0.0, roll(n, -plane))
            xa = jnp.where(x_last, roll(n, LX - 1), roll(n, -1))
            return jnp.where(first, ya, za), jnp.where(first, v, xa)

        for c in range(2):
            v = rs[h, c]
            s_ref[c] = v
            e_ref[c] = zero
            acc[0, c] = zero
            acc[1, c] = zero
            a_ref[0, c], a_ref[1, c] = ahead(v)

        def images():
            sr, si = s_ref[0], s_ref[1]
            gr, gi = signs * sr, signs * si
            gv[0] = gr
            gv[1] = gi
            gv[2] = gr - gi
            back0 = sweep_matrices(0, h, (a_ref[0, 0], a_ref[0, 1]), 0, h, False)
            back2 = sweep_matrices(1, h, (a_ref[1, 0], a_ref[1, 1]), 2, h, True)
            q = []
            for c in range(2):
                b, d = back0[c], back2[c]
                yb = jnp.where(y_first, roll(b, -(LY - 1) * LX), roll(b, LX))
                zb = jnp.where(z_first, 0.0, roll(b, plane))
                xb = jnp.where(x_first, roll(d, -(LX - 1)), roll(d, 1))
                u = gathered(c) + jnp.where(first, yb, zb) + jnp.where(first, 0.0, xb)
                q.append(u + roll(u, half))
            qr, qi = q
            ahead_r, ahead_i = ahead(qr), ahead(qi)
            return sr, si, qr, qi, ahead_r, ahead_i, back0, back2

        def total(v):
            return jnp.sum(jnp.sum(fold(v), axis=0, keepdims=True), axis=1, keepdims=True)

        def scale(k, sr, si, qr, qi):
            numer_real = total(qr * sr + qi * si)
            numer_imag = total(qr * si - qi * sr)
            denom = total(qr * qr + qi * qi) + 2e-6
            live = (lane * 0 + limit) > k
            ar = jnp.where(live, jnp.broadcast_to(numer_real / denom, shape), 0.0)
            ai = jnp.where(live, jnp.broadcast_to(numer_imag / denom, shape), 0.0)
            return ar, ai

        def times(ar, ai, v):
            return ar * v[0] - ai * v[1], ar * v[1] + ai * v[0]

        def step(k, carry):
            sr, si, qr, qi, ahead_r, ahead_i, back0, back2 = images()
            ar, ai = scale(k, sr, si, qr, qi)
            es = times(ar, ai, (sr, si))
            qs = times(ar, ai, (qr, qi))
            for c, old in enumerate((sr, si)):
                e_ref[c] += es[c]
                s_ref[c] = old - qs[c]
            for n, back in enumerate((back0, back2)):
                moved = times(ar, ai, (ahead_r[n], ahead_i[n]))
                added = times(ar, ai, back)
                for c in range(2):
                    a_ref[n, c] -= moved[c]
                    acc[n, c] += added[c]
            return carry

        lax.fori_loop(0, MR_MAX - 1, step, 0)

        def pack(v):
            return jnp.where(low, v[0], v[1])

        def bt_of(v):
            return [-jnp.where(first, v[c], roll(v[c], half)) for c in range(2)]

        def sender(n, where_to, src, dst):
            return pltpu.make_async_remote_copy(
                src_ref=src,
                dst_ref=dst,
                send_sem=ssem.at[ph, n],
                recv_sem=rsem.at[ph, n],
                device_id=where_to,
                device_id_type=MESH,
            )

        target = {"ta": lax.rem(ta + nt + 2 * h - 1, nt)}
        e_old = (e_ref[0], e_ref[1])

        @pl.when(ph == 0)
        def _():
            pl.semaphore_wait(barrier, 4)

        sr, si, qr, qi, _, _, back0, back2 = images()
        ar, ai = scale(MR_MAX - 1, sr, si, qr, qi)
        es = times(ar, ai, (sr, si))
        e_new = [e_old[c] + es[c] for c in range(2)]
        added = times(ar, ai, back2)
        bt = bt_of([acc[1, c] + added[c] for c in range(2)])
        sbuf[ph, 0] = jnp.where(h_is_0, pack(e_new), pack(bt))
        sends = [sender(0, target, sbuf.at[ph, 0], rbuf.at[ph, 0])]
        sends[0].start()
        bs = times(ar, ai, back0)
        bz = []
        for c in range(2):
            v = acc[0, c] + bs[c]
            bz.append(-jnp.where(first, roll(v, half), v))
        sbuf[ph, 1] = pack(e_new)
        sbuf[ph, 2] = pack(bz)
        sends.append(sender(1, {"sa": z_prev}, sbuf.at[ph, 1], rbuf.at[ph, 1]))
        sends.append(sender(2, {"sa": z_next}, sbuf.at[ph, 2], rbuf.at[ph, 2]))
        sends[1].start()
        sends[2].start()

        qs = times(ar, ai, (qr, qi))
        for c, old in enumerate((sr, si)):
            xs[h, c] += e_new[c]
            rs[h, c] = old - qs[c]

        def unpack(n):
            m = rbuf[ph, n]
            w = roll(m, half)
            return jnp.where(low, m, w), jnp.where(low, w, m)

        sends[1].wait()
        sends[2].wait()
        got_e, got_b = unpack(1), unpack(2)

        def hop(times):
            inputs = []
            for c in range(2):
                zin = jnp.where(z_last, roll(got_e[c], -plane), 0.0)
                inputs.append(jnp.where(first, zin, times[c]))
            sweep_matrices(3, other, inputs, None, None, False)
            for c in range(2):
                u = gathered(c)
                zb = jnp.where(z_first, roll(got_b[c], plane), 0.0)
                rs[other, c] += u + roll(u, half) + zb

        @pl.when(h == 0)
        def _():
            for c in range(2):
                rs[1, c] += bt[c]
            sends[0].wait()
            hop(unpack(0))

        @pl.when(h == 1)
        def _():
            hop(e_new)
            sends[0].wait()
            got_t = unpack(0)
            for c in range(2):
                rs[0, c] += got_t[c]

        return token

    lax.fori_loop(0, PHASES, phase, 0)

    for c in range(2):
        x_ref[c] = jnp.where(low, xs[0, c], xs[1, c])
        r_ref[c] = jnp.where(low, rs[0, c], rs[1, c])


def shards(nt, nz, rhs, links, clover, mr_steps):
    dof, lanes = rhs.shape[2], rhs.shape[-1]
    f32 = jnp.float32
    vmem = pl.BlockSpec(memory_space=pltpu.VMEM)
    hbm = pl.BlockSpec(memory_space=pltpu.HBM)
    x, r = pl.pallas_call(
        functools.partial(kernel, nt, nz),
        out_shape=[jax.ShapeDtypeStruct((2, dof, lanes), f32)] * 2,
        in_specs=[hbm, hbm, hbm, hbm],
        out_specs=[vmem, vmem],
        scratch_shapes=[
            pltpu.VMEM((2, dof, lanes), f32),
            pltpu.SMEM((2,), jnp.int32),
            pltpu.VMEM((4, 2, dof, dof, lanes), jnp.bfloat16),
            pltpu.VMEM((2, dof, dof, lanes), jnp.bfloat16),
            pltpu.VMEM((4, 2, 2, dof, dof, lanes), f32),
            pltpu.VMEM((2, 2, dof, lanes), f32),
            pltpu.VMEM((2, 2, dof, lanes), f32),
            pltpu.VMEM((2, dof, lanes), f32),
            pltpu.VMEM((2, dof, lanes), f32),
            pltpu.VMEM((2, 2, dof, lanes), f32),
            pltpu.VMEM((2, 2, dof, lanes), f32),
            pltpu.VMEM((3, dof, lanes), f32),
            pltpu.VMEM((2, 8 * dof, lanes), f32),
            pltpu.VMEM((PHASES, 3, dof, lanes), f32),
            pltpu.VMEM((PHASES, 3, dof, lanes), f32),
            pltpu.SemaphoreType.DMA((7,)),
            pltpu.SemaphoreType.DMA((PHASES, 3)),
            pltpu.SemaphoreType.DMA((PHASES, 3)),
        ],
        compiler_params=pltpu.CompilerParams(
            collective_id=0, has_side_effects=True, vmem_limit_bytes=67043328
        ),
    )(
        rhs.reshape(2, dof, lanes),
        links.reshape(4, 2, dof, dof, lanes),
        clover.reshape(2, dof, dof, lanes),
        mr_steps.reshape(2),
    )
    return x.reshape(rhs.shape), r.reshape(rhs.shape)


def solution(mesh):
    placed = (
        P(None, None, None, "ta", "sa", None),
        P(None, None, None, None, "ta", "sa", None),
        P(None, None, None, "ta", "sa", None),
        P("ta", "sa", None),
    )
    return jax.shard_map(
        functools.partial(shards, mesh.shape["ta"], mesh.shape["sa"]),
        mesh=mesh,
        in_specs=placed,
        out_specs=(P(None, None, None, "ta", "sa", None), P(None, None, None, "ta", "sa", None)),
        check_vma=False,
    )
```

profile of v0, /device:TPU:0, one launch (start us, length us, event | category | flops | bytes accessed | tf_op | source)
XLA Modules:
  0.0 43.5 jit_solution(8879362740740342734)
XLA Ops:
  0.6 40.1 %shard_map.59 = (f32[2,40,128]{2,1,0:T(8,128)}, f32[2,40,128]{2,1,0:T(8,128)}) custom-call(f32[2,40,128]{2,1,0:T(8,128)} %bitcast.12, bf16[4,2,40,40,128]{4,3,2,1,0:T(8,128)(2,1)} %bitcast.10, bf16[2,40,40,128]{3,2,1,0:T(8,128)(2,1)} %bitcast.11, s32[2]{0:T(128)} %bitcast.15), custom_call_target="tpu_custom_call" | custom-call | tf_op jit(solution)/shard_map/pallas_call | solution.py:352
  40.7 1.4 %copy.10 = f32[1,2,40,1,1,128]{5,4,3,2,1,0:T(1,128)} copy(f32[1,2,40,1,1,128]{5,4,3,2,1,0:T(1,128)} %bitcast.14) | data formatting | bytes 81920
  42.1 1.4 %copy.11 = f32[1,2,40,1,1,128]{5,4,3,2,1,0:T(1,128)} copy(f32[1,2,40,1,1,128]{5,4,3,2,1,0:T(1,128)} %bitcast.13) | data formatting | bytes 81920
where the time goes:
time: 43.7 us; the launch traced here: 43.5 us
  Pallas kernels  40.1 us (92%)
  local copies, waits for them, and re-layouts  2.8 us (6%)
  between operations  0.64 us (1%)
    pallas_call x1, Pallas kernels, shards(): pl.pallas_call(functools.partial(kernel, nt, nz), out_shape=[jax.ShapeDty...  40.1 us
    unnamed x2, local copies, waits for them, and re-layouts  2.8 us

commit v1 on v0

v1 whole, which is shorter than its diff:
```python
import functools

import jax
import jax.numpy as jnp
from jax import lax
from jax.experimental import pallas as pl
from jax.experimental.pallas import tpu as pltpu
from jax.sharding import PartitionSpec as P

LZ = 4
LY = 4
LX = 4
MR_MAX = 3
SWEEPS = 2
PHASES = 2 * SWEEPS
PREPARE_UNROLL = 8
MESH = pl.DeviceIdType.MESH
F32 = jnp.float32
BF16 = jnp.bfloat16


def rows_of(dof):
    whole = dof // 16
    return [(16 * t, 16) for t in range(whole)] + [(16 * whole, dof - 16 * whole)]


def kernel(
    nt,
    nz,
    rhs_hbm,
    links_ref,
    clover_ref,
    steps_hbm,
    x_ref,
    r_ref,
    rhs_ref,
    steps_ref,
    lk,
    cl,
    gf,
    gb,
    gh,
    xr,
    rs,
    xs,
    v_ref,
    q_ref,
    s_ref,
    e_ref,
    bs_ref,
    acc,
    t_ref,
    gv,
    opf,
    pk,
    f_ref,
    sbuf,
    rbuf,
    csem,
    ssem,
    rsem,
):
    dof, lanes = rhs_ref.shape[1:]
    half = lanes // 2
    tiles = dof // 8
    whole = dof // 16
    packed = 2 * dof // 16
    pieces = rows_of(dof)
    ta = lax.axis_index("ta")
    sa = lax.axis_index("sa")
    t_next, t_prev = lax.rem(ta + 1, nt), lax.rem(ta + nt - 1, nt)
    z_next, z_prev = lax.rem(sa + 1, nz), lax.rem(sa + nz - 1, nz)

    copies = [
        pltpu.make_async_copy(links_ref.at[d], lk.at[d], csem.at[d]) for d in range(4)
    ] + [
        pltpu.make_async_copy(clover_ref, cl, csem.at[4]),
        pltpu.make_async_copy(rhs_hbm, rhs_ref, csem.at[5]),
        pltpu.make_async_copy(steps_hbm, steps_ref, csem.at[6]),
    ]
    for d in (5, 6, 1, 2, 3, 4, 0):
        copies[d].start()

    barrier = pltpu.get_barrier_semaphore()
    for where_to in ({"ta": t_next}, {"ta": t_prev}, {"sa": z_next}, {"sa": z_prev}):
        pl.semaphore_signal(barrier, inc=1, device_id=where_to, device_id_type=MESH)

    shape = (dof, lanes)
    lane = lax.broadcasted_iota(jnp.int32, shape, 1)
    row = lax.broadcasted_iota(jnp.int32, shape, 0)
    signs = jnp.where(row < dof // 2, 1.0, -1.0).astype(F32)
    low = lane < half
    site = lane % half
    zpos = site // (LY * LX)
    ypos = site // LX % LY
    xpos = site % LX
    z_last, z_first = zpos == LZ - 1, zpos == 0
    y_last, y_first = ypos == LY - 1, ypos == 0
    x_last, x_first = xpos == LX - 1, xpos == 0
    zero = jnp.zeros(shape, F32)
    plane = LY * LX

    def roll(v, by):
        return pltpu.roll(v, by % lanes, 1)

    def first_rows(h, rows):
        at = lax.broadcasted_iota(jnp.int32, (rows, lanes), 1)
        return jnp.where((at >= half) == ((at * 0 + h) == 1), 1.0, 0.0).astype(BF16) > 0.5

    def loop(body):
        def block(outer, carry):
            for inner in range(PREPARE_UNROLL):
                body(outer * PREPARE_UNROLL + inner)
            return carry

        lax.fori_loop(0, dof // PREPARE_UNROLL, block, 0)

    def prepare(h, stage):
        masks = {rows: first_rows(h, rows) for _, rows in pieces}

        def store(ref, i, base, top, c, at, rows, value):
            if rows == 16:
                ref[h, i, base + 16 * whole * c + at : base + 16 * whole * c + at + 16, :] = value
            else:
                ref[h, i, base + 32 * whole + 8 * c : base + 32 * whole + 8 * c + 8, :] = value

        def body(i):
            for c in range(2):
                for at, rows in pieces:
                    cut = slice(at, at + rows)
                    first = masks[rows]
                    if stage == 0:
                        z = pltpu.roll(lk[1, c, i, cut, :], half, 1)
                        g = jnp.where(first, lk[2, c, i, cut, :], z)
                        store(gf, i, 0, 0, c, at, rows, g)
                        store(gb, i, 2 * dof * c, 0, 0, at, rows, g)
                    if stage == 1:
                        x = pltpu.roll(lk[3, c, i, cut, :], half, 1)
                        xr[c, i, cut, :] = x
                        store(gf, i, 2 * dof, 0, c, at, rows, jnp.where(first, cl[c, i, cut, :], x))
                    if stage == 2:
                        g = jnp.where(first, lk[0, c, i, cut, :], xr[c, i, cut, :])
                        store(gb, i, 2 * dof * c, 0, 1, at, rows, g)
                    if stage == 3:
                        z = pltpu.roll(lk[1, c, i, cut, :], half, 1)
                        store(gh, i, 0, 0, c, at, rows, jnp.where(first, lk[0, c, i, cut, :], z))

        loop(body)

    copies[5].wait()
    for c in range(2):
        v = rhs_ref[c]
        w = roll(v, half)
        rs[0, c] = jnp.where(low, v, w)
        rs[1, c] = jnp.where(low, w, v)
        xs[0, c] = zero
        xs[1, c] = zero

    for stage, needs in enumerate(((1, 2), (3, 4), (0, 6))):
        for d in needs:
            copies[d].wait()
        prepare(sa % 2, stage)

    def fold(v):
        total = v[0:8]
        for t in range(1, tiles):
            total = total + v[8 * t : 8 * t + 8]
        return total

    def gathered(slot):
        parts = []
        for t in range(tiles):
            total = None
            for k in range(8):
                piece = f_ref[slot, pl.ds(8 * 8 * t + k, 8, stride=8), :]
                total = piece if total is None else total + piece
            parts.append(total)
        return jnp.concatenate(parts, axis=0)

    def two(v):
        high = v.astype(BF16).astype(F32)
        return high, v - high

    def put_operands(slot, group, vr, vi):
        for term, (r, i) in enumerate(zip(two(vr), two(vi))):
            n = -i
            top = 16 * whole
            out = [r[16 * t : 16 * t + 16] for t in range(whole)]
            out += [i[16 * t : 16 * t + 16] for t in range(whole)]
            out += [n[16 * t : 16 * t + 16] for t in range(whole)]
            out += [jnp.concatenate([r[top:], n[top:]], axis=0), jnp.concatenate([i[top:], r[top:]], axis=0)]
            for at, value in enumerate(out):
                opf[slot, group, term, at] = value.astype(BF16)

    def forward(slot, groups, matrix):
        def operand(group, term, at):
            return opf[slot, group, term, at].astype(F32)

        real = list(range(whole)) + list(range(2 * whole, 3 * whole)) + [3 * whole]
        imag = list(range(whole, 2 * whole)) + list(range(whole)) + [3 * whole + 1]
        for o in range(dof):
            sums = [None, None]
            for group in range(groups):
                for t in range(packed):
                    m = matrix(o, group, t).astype(F32)
                    for term in range(2):
                        for part, order in enumerate((real, imag)):
                            p = m * operand(group, term, order[t])
                            sums[part] = p if sums[part] is None else sums[part] + p
            for part in range(2):
                f_ref[part, 8 * o : 8 * o + 8, :] = sums[part][0:8] + sums[part][8:16]

    def backward(slot, matrix):
        rounds = []
        t = 0
        while t + 1 < packed:
            rounds.append([(t, 0, dof), (t + 1, 0, dof)])
            t += 2
        if t < packed:
            rounds.append([(t, 0, dof // 2), (t, dof // 2, dof)])
        done = {}
        for index, chains in enumerate(rounds):
            sums = [[None, None] for _ in chains]
            for step in range(chains[0][2] - chains[0][1]):
                if index == 0:
                    for n in range(6):
                        spread = jnp.broadcast_to(gv[n, pl.ds(step, 1), :], (16, lanes))
                        pk[slot, n, step] = spread.astype(BF16)
                for chain, (t, start, _) in enumerate(chains):
                    i = start + step
                    mr = matrix(i, 0, t).astype(F32)
                    mi = matrix(i, 1, t).astype(F32)
                    x = [pk[slot, n, i].astype(F32) for n in range(6)]
                    for part, terms in enumerate(
                        (
                            ((mr, x[0]), (mr, x[1]), (mi, x[2]), (mi, x[3])),
                            ((mr, x[2]), (mr, x[3]), (mi, x[4]), (mi, x[5])),
                        )
                    ):
                        for m, y in terms:
                            p = m * y
                            old = sums[chain][part]
                            sums[chain][part] = p if old is None else old + p
            for chain, (t, _, _) in enumerate(chains):
                if t in done:
                    done[t] = [a + b for a, b in zip(done[t], sums[chain])]
                else:
                    done[t] = sums[chain]
        out = []
        for group in range(2):
            out.append([])
            for part in range(2):
                parts = [done[whole * group + t][part] for t in range(whole)]
                parts.append(done[2 * whole][part][8 * group : 8 * group + 8])
                out[group].append(-signs * jnp.concatenate(parts, axis=0))
        return out

    def phase(ph, token):
        h = lax.rem(ph + sa, 2)
        other = 1 - h
        limit = steps_ref[h]
        first = (lane >= half) == ((lane * 0 + h) == 1)
        h_is_0 = (lane * 0 + h) == 0

        def ahead(v):
            n = -v
            ya = jnp.where(y_last, roll(n, (LY - 1) * LX), roll(n, -LX))
            za = jnp.where(z_last, 0.0, roll(n, -plane))
            xa = jnp.where(x_last, roll(n, LX - 1), roll(n, -1))
            return jnp.where(first, ya, za), jnp.where(first, v, xa)

        for c in range(2):
            v = rs[h, c]
            v_ref[c] = v
            s_ref[c] = v
            e_ref[c] = v
            q_ref[c] = zero
            for n in range(2):
                acc[n, c] = zero
                bs_ref[n, c] = zero

        def total(v):
            return jnp.sum(jnp.sum(fold(v), axis=0, keepdims=True), axis=1, keepdims=True)

        def scale(k):
            qr, qi, sr, si = q_ref[0], q_ref[1], s_ref[0], s_ref[1]
            numer_real = total(qr * sr + qi * si)
            numer_imag = total(qr * si - qi * sr)
            denom = total(qr * qr + qi * qi) + 2e-6
            live = (lane * 0 + limit) > k
            ar = jnp.where(live, jnp.broadcast_to(numer_real / denom, shape), 0.0)
            ai = jnp.where(live, jnp.broadcast_to(numer_imag / denom, shape), 0.0)
            return ar, ai

        def times(ar, ai, v):
            return ar * v[0] - ai * v[1], ar * v[1] + ai * v[0]

        def step(k, carry):
            ar, ai = scale(k - 1)
            opening = (lane * 0 + k) == 0
            ar = jnp.where(opening, -1.0, ar)
            ai = jnp.where(opening, 0.0, ai)

            vr, vi = v_ref[0], v_ref[1]
            gr, gi = two(signs * vr), two(signs * vi)
            for term in range(2):
                gv[term] = gr[term]
                gv[2 + term] = gi[term]
                gv[4 + term] = -gr[term]

            aheads = [ahead(vr), ahead(vi)]
            for group in range(2):
                put_operands(k, group, aheads[0][group], aheads[1][group])

            back0, back2 = backward(
                k, lambda i, c, t: gb[h, i, 2 * dof * c + 16 * t : 2 * dof * c + 16 * t + 16, :]
            )
            near, moved = [], []
            for c in range(2):
                b, d = back0[c], back2[c]
                yb = jnp.where(y_first, roll(b, -(LY - 1) * LX), roll(b, LX))
                zb = jnp.where(z_first, 0.0, roll(b, plane))
                xb = jnp.where(x_first, roll(d, -(LX - 1)), roll(d, 1))
                u = jnp.where(first, yb, zb) + jnp.where(first, 0.0, xb)
                near.append(u + roll(u, half))
                moved.append((jnp.where(first, roll(b, half), b), jnp.where(first, d, roll(d, half))))

            forward(
                k,
                2,
                lambda o, group, t: gf[h, o, 2 * dof * group + 16 * t : 2 * dof * group + 16 * t + 16, :],
            )

            old_s = (s_ref[0], s_ref[1])
            old_q = (q_ref[0], q_ref[1])
            es = times(ar, ai, old_s)
            qs = times(ar, ai, old_q)
            for c in range(2):
                e_ref[c] += es[c]
                s_ref[c] = old_s[c] - qs[c]
            for n in range(2):
                old_b = (bs_ref[n, 0], bs_ref[n, 1])
                now = (moved[0][n], moved[1][n])
                added = times(ar, ai, old_b)
                taken = times(ar, ai, now)
                for c in range(2):
                    acc[n, c] += added[c]
                    bs_ref[n, c] = old_b[c] - taken[c]
            w = []
            for c in range(2):
                u = gathered(c)
                w.append(u + roll(u, half) + near[c])
            ws = times(ar, ai, w)
            for c in range(2):
                q = old_q[c] - ws[c]
                q_ref[c] = q
                v_ref[c] = q
            return carry

        lax.fori_loop(0, MR_MAX, step, 0)

        def pack(v):
            return jnp.where(low, v[0], v[1])

        def sender(n, where_to, src, dst):
            return pltpu.make_async_remote_copy(
                src_ref=src,
                dst_ref=dst,
                send_sem=ssem.at[ph, n],
                recv_sem=rsem.at[ph, n],
                device_id=where_to,
                device_id_type=MESH,
            )

        target = {"ta": lax.rem(ta + nt + 2 * h - 1, nt)}

        @pl.when(ph == 0)
        def _():
            pl.semaphore_wait(barrier, 4)

        ar, ai = scale(MR_MAX - 1)
        es = times(ar, ai, (s_ref[0], s_ref[1]))
        e_new = [e_ref[c] + es[c] for c in range(2)]
        added = times(ar, ai, (bs_ref[1, 0], bs_ref[1, 1]))
        bt = [-(acc[1, c] + added[c]) for c in range(2)]
        sbuf[ph, 0] = jnp.where(h_is_0, pack(e_new), pack(bt))
        sends = [sender(0, target, sbuf.at[ph, 0], rbuf.at[ph, 0])]
        sends[0].start()
        bs = times(ar, ai, (bs_ref[0, 0], bs_ref[0, 1]))
        bz = [-(acc[0, c] + bs[c]) for c in range(2)]
        sbuf[ph, 1] = pack(e_new)
        sbuf[ph, 2] = pack(bz)
        sends.append(sender(1, {"sa": z_prev}, sbuf.at[ph, 1], rbuf.at[ph, 1]))
        sends.append(sender(2, {"sa": z_next}, sbuf.at[ph, 2], rbuf.at[ph, 2]))
        sends[1].start()
        sends[2].start()

        qs = times(ar, ai, (q_ref[0], q_ref[1]))
        for c in range(2):
            xs[h, c] += e_new[c]
            rs[h, c] = s_ref[c] - qs[c]

        @pl.when(h == 0)
        def _():
            for c in range(2):
                rs[1, c] += bt[c]

        @pl.when(h == 1)
        def _():
            for c in range(2):
                t_ref[c] = e_new[c]

        @pl.when(ph == 0)
        def _():
            for stage in range(4):
                prepare(other, stage)
            prepare(h, 3)

        def unpack(n):
            m = rbuf[ph, n]
            w = roll(m, half)
            return jnp.where(low, m, w), jnp.where(low, w, m)

        sends[1].wait()
        sends[2].wait()
        got_b = unpack(2)
        for c in range(2):
            rs[other, c] += jnp.where(z_first, roll(got_b[c], plane), 0.0)

        @pl.when(h == 0)
        def _():
            sends[0].wait()
            got_t = unpack(0)
            for c in range(2):
                t_ref[c] = got_t[c]

        got_e = unpack(1)
        inputs = []
        for c in range(2):
            zin = jnp.where(z_last, roll(got_e[c], -plane), 0.0)
            inputs.append(jnp.where(first, zin, t_ref[c]))
        slot = lax.rem(ph, MR_MAX)
        put_operands(slot, 0, inputs[0], inputs[1])
        forward(slot, 1, lambda o, group, t: gh[other, o, 16 * t : 16 * t + 16, :])
        for c in range(2):
            u = gathered(c)
            rs[other, c] += u + roll(u, half)

        @pl.when(h == 1)
        def _():
            sends[0].wait()
            got_t = unpack(0)
            for c in range(2):
                rs[0, c] += got_t[c]

        return token

    lax.fori_loop(0, PHASES, phase, 0)

    for c in range(2):
        x_ref[c] = jnp.where(low, xs[0, c], xs[1, c])
        r_ref[c] = jnp.where(low, rs[0, c], rs[1, c])


def shards(nt, nz, rhs, links, clover, mr_steps):
    dof, lanes = rhs.shape[2], rhs.shape[-1]
    vmem = pl.BlockSpec(memory_space=pltpu.VMEM)
    hbm = pl.BlockSpec(memory_space=pltpu.HBM)
    operands = 3 * (dof // 16) + 2
    field = pltpu.VMEM((2, dof, lanes), F32)
    fields = pltpu.VMEM((2, 2, dof, lanes), F32)
    x, r = pl.pallas_call(
        functools.partial(kernel, nt, nz),
        out_shape=[jax.ShapeDtypeStruct((2, dof, lanes), F32)] * 2,
        in_specs=[hbm, hbm, hbm, hbm],
        out_specs=[vmem, vmem],
        scratch_shapes=[
            field,
            pltpu.SMEM((2,), jnp.int32),
            pltpu.VMEM((4, 2, dof, dof, lanes), BF16),
            pltpu.VMEM((2, dof, dof, lanes), BF16),
            pltpu.VMEM((2, dof, 4 * dof, lanes), BF16),
            pltpu.VMEM((2, dof, 4 * dof, lanes), BF16),
            pltpu.VMEM((2, dof, 2 * dof, lanes), BF16),
            pltpu.VMEM((2, dof, dof, lanes), BF16),
            fields,
            fields,
            field,
            field,
            field,
            field,
            fields,
            fields,
            field,
            pltpu.VMEM((6, dof, lanes), F32),
            pltpu.VMEM((MR_MAX, 2, 2, operands, 16, lanes), BF16),
            pltpu.VMEM((MR_MAX, 6, dof, 16, lanes), BF16),
            pltpu.VMEM((2, 8 * dof, lanes), F32),
            pltpu.VMEM((PHASES, 3, dof, lanes), F32),
            pltpu.VMEM((PHASES, 3, dof, lanes), F32),
            pltpu.SemaphoreType.DMA((7,)),
            pltpu.SemaphoreType.DMA((PHASES, 3)),
            pltpu.SemaphoreType.DMA((PHASES, 3)),
        ],
        compiler_params=pltpu.CompilerParams(
            collective_id=0, has_side_effects=True, vmem_limit_bytes=67043328
        ),
    )(
        rhs.reshape(2, dof, lanes),
        links.reshape(4, 2, dof, dof, lanes),
        clover.reshape(2, dof, dof, lanes),
        mr_steps.reshape(2),
    )
    return x.reshape(rhs.shape), r.reshape(rhs.shape)


def solution(mesh):
    placed = (
        P(None, None, None, "ta", "sa", None),
        P(None, None, None, None, "ta", "sa", None),
        P(None, None, None, "ta", "sa", None),
        P("ta", "sa", None),
    )
    return jax.shard_map(
        functools.partial(shards, mesh.shape["ta"], mesh.shape["sa"]),
        mesh=mesh,
        in_specs=placed,
        out_specs=(P(None, None, None, "ta", "sa", None), P(None, None, None, "ta", "sa", None)),
        check_vma=False,
    )
```

time: 43.7 us -> 40.4 us (0.924)
  Pallas kernels: 40.1 us -> 36.7 us
    pallas_call x1, Pallas kernels: 40.1 us -> 36.7 us  [shards(): pl.pallas_call(functools.partial(kernel, nt, nz), out_shape=[jax.ShapeDty...]
where the time goes in v1:
time: 40.4 us; the launch traced here: 40.1 us
  Pallas kernels  36.7 us (91%)
  local copies, waits for them, and re-layouts  2.8 us (7%)
  between operations  0.64 us (2%)
    pallas_call x1, Pallas kernels, shards(): pl.pallas_call(functools.partial(kernel, nt, nz), out_shape=[jax.ShapeDty...  36.7 us
    unnamed x2, local copies, waits for them, and re-layouts  2.8 us

profile of v1, /device:TPU:0, one launch (start us, length us, event | category | flops | bytes accessed | tf_op | source)
XLA Modules:
  0.0 40.1 jit_solution(10110921907967399835)
XLA Ops:
  0.6 36.7 %shard_map.59 = (f32[2,40,128]{2,1,0:T(8,128)}, f32[2,40,128]{2,1,0:T(8,128)}) custom-call(f32[2,40,128]{2,1,0:T(8,128)} %bitcast.12, bf16[4,2,40,40,128]{4,3,2,1,0:T(8,128)(2,1)} %bitcast.10, bf16[2,40,40,128]{3,2,1,0:T(8,128)(2,1)} %bitcast.11, s32[2]{0:T(128)} %bitcast.15), custom_call_target="tpu_custom_call" | custom-call | tf_op jit(solution)/shard_map/pallas_call | solution.py:472
  37.3 1.4 %copy.10 = f32[1,2,40,1,1,128]{5,4,3,2,1,0:T(1,128)} copy(f32[1,2,40,1,1,128]{5,4,3,2,1,0:T(1,128)} %bitcast.14) | data formatting | bytes 81920
  38.7 1.4 %copy.11 = f32[1,2,40,1,1,128]{5,4,3,2,1,0:T(1,128)} copy(f32[1,2,40,1,1,128]{5,4,3,2,1,0:T(1,128)} %bitcast.13) | data formatting | bytes 81920

commit v2 on v1

--- a/solution.py
+++ b/solution.py
@@ -13,7 +13,7 @@
 MR_MAX = 3
 SWEEPS = 2
 PHASES = 2 * SWEEPS
-PREPARE_UNROLL = 8
+PREPARE_UNROLL = 20
 MESH = pl.DeviceIdType.MESH
 F32 = jnp.float32
 BF16 = jnp.bfloat16
@@ -43,13 +43,14 @@
     xr,
     rs,
     xs,
-    v_ref,
     q_ref,
     s_ref,
     e_ref,
     bs_ref,
     acc,
+    bm_ref,
     t_ref,
+    z_ref,
     gv,
     opf,
     pk,
@@ -167,12 +168,12 @@
             total = total + v[8 * t : 8 * t + 8]
         return total
 
-    def gathered(slot):
+    def gathered(slot, part):
         parts = []
         for t in range(tiles):
             total = None
             for k in range(8):
-                piece = f_ref[slot, pl.ds(8 * 8 * t + k, 8, stride=8), :]
+                piece = f_ref[slot, part, pl.ds(8 * 8 * t + k, 8, stride=8), :]
                 total = piece if total is None else total + piece
             parts.append(total)
         return jnp.concatenate(parts, axis=0)
@@ -208,9 +209,9 @@
                             p = m * operand(group, term, order[t])
                             sums[part] = p if sums[part] is None else sums[part] + p
             for part in range(2):
-                f_ref[part, 8 * o : 8 * o + 8, :] = sums[part][0:8] + sums[part][8:16]
-
-    def backward(slot, matrix):
+                f_ref[slot, part, 8 * o : 8 * o + 8, :] = sums[part][0:8] + sums[part][8:16]
+
+    def backward(slot, k, matrix):
         rounds = []
         t = 0
         while t + 1 < packed:
@@ -224,7 +225,7 @@
             for step in range(chains[0][2] - chains[0][1]):
                 if index == 0:
                     for n in range(6):
-                        spread = jnp.broadcast_to(gv[n, pl.ds(step, 1), :], (16, lanes))
+                        spread = jnp.broadcast_to(gv[k, n, pl.ds(step, 1), :], (16, lanes))
                         pk[slot, n, step] = spread.astype(BF16)
                 for chain, (t, start, _) in enumerate(chains):
                     i = start + step
@@ -269,53 +270,50 @@
             xa = jnp.where(x_last, roll(n, LX - 1), roll(n, -1))
             return jnp.where(first, ya, za), jnp.where(first, v, xa)
 
-        for c in range(2):
-            v = rs[h, c]
-            v_ref[c] = v
-            s_ref[c] = v
-            e_ref[c] = v
-            q_ref[c] = zero
-            for n in range(2):
-                acc[n, c] = zero
-                bs_ref[n, c] = zero
-
         def total(v):
             return jnp.sum(jnp.sum(fold(v), axis=0, keepdims=True), axis=1, keepdims=True)
 
-        def scale(k):
-            qr, qi, sr, si = q_ref[0], q_ref[1], s_ref[0], s_ref[1]
-            numer_real = total(qr * sr + qi * si)
-            numer_imag = total(qr * si - qi * sr)
-            denom = total(qr * qr + qi * qi) + 2e-6
-            live = (lane * 0 + limit) > k
-            ar = jnp.where(live, jnp.broadcast_to(numer_real / denom, shape), 0.0)
-            ai = jnp.where(live, jnp.broadcast_to(numer_imag / denom, shape), 0.0)
+        def scale(k, q, s):
+            numer_real = total(q[0] * s[0] + q[1] * s[1])
+            numer_imag = total(q[0] * s[1] - q[1] * s[0])
+            denom = total(q[0] * q[0] + q[1] * q[1]) + 2e-6
+            live = (lane[0:1] * 0 + limit) > k
+            ar = jnp.where(live, jnp.broadcast_to(numer_real / denom, (1, lanes)), 0.0)
+            ai = jnp.where(live, jnp.broadcast_to(numer_imag / denom, (1, lanes)), 0.0)
             return ar, ai
 
-        def times(ar, ai, v):
-            return ar * v[0] - ai * v[1], ar * v[1] + ai * v[0]
-
-        def step(k, carry):
-            ar, ai = scale(k - 1)
-            opening = (lane * 0 + k) == 0
-            ar = jnp.where(opening, -1.0, ar)
-            ai = jnp.where(opening, 0.0, ai)
-
-            vr, vi = v_ref[0], v_ref[1]
-            gr, gi = two(signs * vr), two(signs * vi)
+        def times(a, v):
+            return [a[0] * v[0] - a[1] * v[1], a[0] * v[1] + a[1] * v[0]]
+
+        def plus(u, v):
+            return [u[0] + v[0], u[1] + v[1]]
+
+        def minus(u, v):
+            return [u[0] - v[0], u[1] - v[1]]
+
+        def keep(ref, v):
+            for c in range(2):
+                ref[c] = v[c]
+
+        def kept(ref):
+            return [ref[0], ref[1]]
+
+        def apply(k, v):
+            slot = lax.rem(ph + k, MR_MAX)
+            gr, gi = two(signs * v[0]), two(signs * v[1])
             for term in range(2):
-                gv[term] = gr[term]
-                gv[2 + term] = gi[term]
-                gv[4 + term] = -gr[term]
-
-            aheads = [ahead(vr), ahead(vi)]
+                gv[k, term] = gr[term]
+                gv[k, 2 + term] = gi[term]
+                gv[k, 4 + term] = -gr[term]
+            aheads = [ahead(v[0]), ahead(v[1])]
             for group in range(2):
-                put_operands(k, group, aheads[0][group], aheads[1][group])
-
+                put_operands(slot, group, aheads[0][group], aheads[1][group])
             back0, back2 = backward(
-                k, lambda i, c, t: gb[h, i, 2 * dof * c + 16 * t : 2 * dof * c + 16 * t + 16, :]
+                slot,
+                k,
+                lambda i, c, t: gb[h, i, 2 * dof * c + 16 * t : 2 * dof * c + 16 * t + 16, :],
             )
-            near, moved = [], []
+            near = []
             for c in range(2):
                 b, d = back0[c], back2[c]
                 yb = jnp.where(y_first, roll(b, -(LY - 1) * LX), roll(b, LX))
@@ -323,41 +321,44 @@
                 xb = jnp.where(x_first, roll(d, -(LX - 1)), roll(d, 1))
                 u = jnp.where(first, yb, zb) + jnp.where(first, 0.0, xb)
                 near.append(u + roll(u, half))
-                moved.append((jnp.where(first, roll(b, half), b), jnp.where(first, d, roll(d, half))))
-
+                bm_ref[k, 0, c] = jnp.where(first, roll(b, half), b)
+                bm_ref[k, 1, c] = jnp.where(first, d, roll(d, half))
             forward(
-                k,
+                slot,
                 2,
                 lambda o, group, t: gf[h, o, 2 * dof * group + 16 * t : 2 * dof * group + 16 * t + 16, :],
             )
-
-            old_s = (s_ref[0], s_ref[1])
-            old_q = (q_ref[0], q_ref[1])
-            es = times(ar, ai, old_s)
-            qs = times(ar, ai, old_q)
-            for c in range(2):
-                e_ref[c] += es[c]
-                s_ref[c] = old_s[c] - qs[c]
-            for n in range(2):
-                old_b = (bs_ref[n, 0], bs_ref[n, 1])
-                now = (moved[0][n], moved[1][n])
-                added = times(ar, ai, old_b)
-                taken = times(ar, ai, now)
-                for c in range(2):
-                    acc[n, c] += added[c]
-                    bs_ref[n, c] = old_b[c] - taken[c]
-            w = []
-            for c in range(2):
-                u = gathered(c)
-                w.append(u + roll(u, half) + near[c])
-            ws = times(ar, ai, w)
-            for c in range(2):
-                q = old_q[c] - ws[c]
-                q_ref[c] = q
-                v_ref[c] = q
-            return carry
-
-        lax.fori_loop(0, MR_MAX, step, 0)
+            out = []
+            for c in range(2):
+                u = gathered(slot, c)
+                out.append(u + roll(u, half) + near[c])
+            return out
+
+        s = kept(rs.at[h])
+        q = apply(0, s)
+        alpha = scale(0, q, s)
+        w = apply(1, q)
+        e = times(alpha, s)
+        s = minus(s, times(alpha, q))
+        q = minus(q, times(alpha, w))
+        keep(e_ref, e)
+        keep(s_ref, s)
+        keep(q_ref, q)
+        for n in range(2):
+            b = kept(bm_ref.at[0, n])
+            keep(acc.at[n], times(alpha, b))
+            keep(bs_ref.at[n], minus(b, times(alpha, kept(bm_ref.at[1, n]))))
+        alpha = scale(1, q, s)
+        w = apply(2, q)
+        s, q = kept(s_ref), kept(q_ref)
+        e = plus(kept(e_ref), times(alpha, s))
+        s = minus(s, times(alpha, q))
+        q = minus(q, times(alpha, w))
+        back = []
+        for n in range(2):
+            b = kept(bs_ref.at[n])
+            total_b = plus(kept(acc.at[n]), times(alpha, b))
+            back.append((total_b, minus(b, times(alpha, kept(bm_ref.at[2, n])))))
 
         def pack(v):
             return jnp.where(low, v[0], v[1])
@@ -378,16 +379,13 @@
         def _():
             pl.semaphore_wait(barrier, 4)
 
-        ar, ai = scale(MR_MAX - 1)
-        es = times(ar, ai, (s_ref[0], s_ref[1]))
-        e_new = [e_ref[c] + es[c] for c in range(2)]
-        added = times(ar, ai, (bs_ref[1, 0], bs_ref[1, 1]))
-        bt = [-(acc[1, c] + added[c]) for c in range(2)]
+        alpha = scale(2, q, s)
+        e_new = plus(e, times(alpha, s))
+        bt = [-v for v in plus(back[1][0], times(alpha, back[1][1]))]
         sbuf[ph, 0] = jnp.where(h_is_0, pack(e_new), pack(bt))
         sends = [sender(0, target, sbuf.at[ph, 0], rbuf.at[ph, 0])]
         sends[0].start()
-        bs = times(ar, ai, (bs_ref[0, 0], bs_ref[0, 1]))
-        bz = [-(acc[0, c] + bs[c]) for c in range(2)]
+        bz = [-v for v in plus(back[0][0], times(alpha, back[0][1]))]
         sbuf[ph, 1] = pack(e_new)
         sbuf[ph, 2] = pack(bz)
         sends.append(sender(1, {"sa": z_prev}, sbuf.at[ph, 1], rbuf.at[ph, 1]))
@@ -395,10 +393,10 @@
         sends[1].start()
         sends[2].start()
 
-        qs = times(ar, ai, (q_ref[0], q_ref[1]))
+        left = minus(s, times(alpha, q))
         for c in range(2):
             xs[h, c] += e_new[c]
-            rs[h, c] = s_ref[c] - qs[c]
+            rs[h, c] = left[c]
 
         @pl.when(h == 0)
         def _():
@@ -423,27 +421,32 @@
 
         sends[1].wait()
         sends[2].wait()
-        got_b = unpack(2)
+        m = rbuf[ph, 2]
+        near_low, near_high = roll(m, half + plane), roll(m, plane)
+        rs[other, 0] += jnp.where(z_first, jnp.where(low, near_low, near_high), 0.0)
+        rs[other, 1] += jnp.where(z_first, jnp.where(low, near_high, near_low), 0.0)
+        m = rbuf[ph, 1]
+        own, far = roll(m, half - plane), roll(m, -plane)
+        zin = (
+            jnp.where(z_last, jnp.where(h_is_0, own, far), 0.0),
+            jnp.where(z_last, jnp.where(h_is_0, far, own), 0.0),
+        )
         for c in range(2):
-            rs[other, c] += jnp.where(z_first, roll(got_b[c], plane), 0.0)
+            z_ref[c] = zin[c]
 
         @pl.when(h == 0)
         def _():
             sends[0].wait()
-            got_t = unpack(0)
-            for c in range(2):
-                t_ref[c] = got_t[c]
-
-        got_e = unpack(1)
-        inputs = []
-        for c in range(2):
-            zin = jnp.where(z_last, roll(got_e[c], -plane), 0.0)
-            inputs.append(jnp.where(first, zin, t_ref[c]))
+            m = rbuf[ph, 0]
+            t_ref[0] = roll(m, half)
+            t_ref[1] = m
+
+        inputs = [jnp.where(first, z_ref[c], t_ref[c]) for c in range(2)]
         slot = lax.rem(ph, MR_MAX)
         put_operands(slot, 0, inputs[0], inputs[1])
         forward(slot, 1, lambda o, group, t: gh[other, o, 16 * t : 16 * t + 16, :])
         for c in range(2):
-            u = gathered(c)
+            u = gathered(slot, c)
             rs[other, c] += u + roll(u, half)
 
         @pl.when(h == 1)
@@ -488,14 +491,15 @@
             field,
             field,
             field,
-            field,
             fields,
             fields,
+            pltpu.VMEM((MR_MAX, 2, 2, dof, lanes), F32),
             field,
-            pltpu.VMEM((6, dof, lanes), F32),
+            field,
+            pltpu.VMEM((MR_MAX, 6, dof, lanes), F32),
             pltpu.VMEM((MR_MAX, 2, 2, operands, 16, lanes), BF16),
             pltpu.VMEM((MR_MAX, 6, dof, 16, lanes), BF16),
-            pltpu.VMEM((2, 8 * dof, lanes), F32),
+            pltpu.VMEM((MR_MAX, 2, 8 * dof, lanes), F32),
             pltpu.VMEM((PHASES, 3, dof, lanes), F32),
             pltpu.VMEM((PHASES, 3, dof, lanes), F32),
             pltpu.SemaphoreType.DMA((7,)),

time: 40.4 us -> 37.9 us (0.938)
  Pallas kernels: 36.7 us -> 34.2 us
    pallas_call x1, Pallas kernels: 36.7 us -> 34.2 us  [shards(): pl.pallas_call(functools.partial(kernel, nt, nz), out_shape=[jax.ShapeDty...]
where the time goes in v2:
time: 37.9 us; the launch traced here: 37.7 us
  Pallas kernels  34.2 us (90%)
  local copies, waits for them, and re-layouts  2.8 us (7%)
  between operations  0.64 us (2%)
    pallas_call x1, Pallas kernels, shards(): pl.pallas_call(functools.partial(kernel, nt, nz), out_shape=[jax.ShapeDty...  34.2 us
    unnamed x2, local copies, waits for them, and re-layouts  2.8 us

profile of v2, /device:TPU:0, one launch (start us, length us, event | category | flops | bytes accessed | tf_op | source)
XLA Modules:
  0.0 37.7 jit_solution(2219378260786336480)
XLA Ops:
  0.6 34.2 %shard_map.59 = (f32[2,40,128]{2,1,0:T(8,128)}, f32[2,40,128]{2,1,0:T(8,128)}) custom-call(f32[2,40,128]{2,1,0:T(8,128)} %bitcast.12, bf16[4,2,40,40,128]{4,3,2,1,0:T(8,128)(2,1)} %bitcast.10, bf16[2,40,40,128]{3,2,1,0:T(8,128)(2,1)} %bitcast.11, s32[2]{0:T(128)} %bitcast.15), custom_call_target="tpu_custom_call" | custom-call | tf_op jit(solution)/shard_map/pallas_call | solution.py:475
  34.9 1.4 %copy.10 = f32[1,2,40,1,1,128]{5,4,3,2,1,0:T(1,128)} copy(f32[1,2,40,1,1,128]{5,4,3,2,1,0:T(1,128)} %bitcast.14) | data formatting | bytes 81920
  36.3 1.4 %copy.11 = f32[1,2,40,1,1,128]{5,4,3,2,1,0:T(1,128)} copy(f32[1,2,40,1,1,128]{5,4,3,2,1,0:T(1,128)} %bitcast.13) | data formatting | bytes 81920

commit v3 on v2

--- a/solution.py
+++ b/solution.py
@@ -31,8 +31,7 @@
     links_ref,
     clover_ref,
     steps_hbm,
-    x_ref,
-    r_ref,
+    out_ref,
     rhs_ref,
     steps_ref,
     lk,
@@ -461,8 +460,8 @@
     lax.fori_loop(0, PHASES, phase, 0)
 
     for c in range(2):
-        x_ref[c] = jnp.where(low, xs[0, c], xs[1, c])
-        r_ref[c] = jnp.where(low, rs[0, c], rs[1, c])
+        out_ref[0, c] = jnp.where(low, xs[0, c], xs[1, c])
+        out_ref[1, c] = jnp.where(low, rs[0, c], rs[1, c])
 
 
 def shards(nt, nz, rhs, links, clover, mr_steps):
@@ -472,11 +471,11 @@
     operands = 3 * (dof // 16) + 2
     field = pltpu.VMEM((2, dof, lanes), F32)
     fields = pltpu.VMEM((2, 2, dof, lanes), F32)
-    x, r = pl.pallas_call(
+    out = pl.pallas_call(
         functools.partial(kernel, nt, nz),
-        out_shape=[jax.ShapeDtypeStruct((2, dof, lanes), F32)] * 2,
+        out_shape=jax.ShapeDtypeStruct((2, 2, dof, lanes), F32),
         in_specs=[hbm, hbm, hbm, hbm],
-        out_specs=[vmem, vmem],
+        out_specs=vmem,
         scratch_shapes=[
             field,
             pltpu.SMEM((2,), jnp.int32),
@@ -515,7 +514,7 @@
         clover.reshape(2, dof, dof, lanes),
         mr_steps.reshape(2),
     )
-    return x.reshape(rhs.shape), r.reshape(rhs.shape)
+    return out[0].reshape(rhs.shape), out[1].reshape(rhs.shape)
 
 
 def solution(mesh):

time: 37.9 us -> 36.5 us (0.963)
  local copies, waits for them, and re-layouts: 2.8 us -> 1.43 us
    unnamed x2 -> x0, local copies, waits for them, and re-layouts: 2.8 us -> none
    slice x0 -> x1, local copies, waits for them, and re-layouts: none -> 1.43 us  [shards(): return (out[0].reshape(rhs.shape), out[1].reshape(rhs.shape))]
where the time goes in v3:
time: 36.5 us; the launch traced here: 36.3 us
  Pallas kernels  34.2 us (94%)
  local copies, waits for them, and re-layouts  1.43 us (4%)
  between operations  0.64 us (2%)
    pallas_call x1, Pallas kernels, shards(): pl.pallas_call(functools.partial(kernel, nt, nz), out_shape=jax.ShapeDtyp...  34.2 us
    slice x1, local copies, waits for them, and re-layouts, shards(): return (out[0].reshape(rhs.shape), out[1].reshape(rhs.shape))  1.43 us

profile of v3, /device:TPU:0, one launch (start us, length us, event | category | flops | bytes accessed | tf_op | source)
XLA Modules:
  0.0 36.3 jit_solution(14177056874160037514)
XLA Ops:
  0.6 34.2 %shard_map.59 = f32[2,2,40,128]{3,2,1,0:T(8,128)} custom-call(f32[2,40,128]{2,1,0:T(8,128)} %bitcast.12, bf16[4,2,40,40,128]{4,3,2,1,0:T(8,128)(2,1)} %bitcast.10, bf16[2,40,40,128]{3,2,1,0:T(8,128)(2,1)} %bitcast.11, s32[2]{0:T(128)} %bitcast.15), custom_call_target="tpu_custom_call" | custom-call | tf_op jit(solution)/shard_map/pallas_call | solution.py:474
  34.9 1.4 %fusion = (f32[1,2,40,128]{3,2,1,0:T(8,128)}, f32[1,2,40,128]{3,2,1,0:T(8,128)}) fusion(f32[2,2,40,128]{3,2,1,0:T(8,128)} %shard_map.59), kind=kLoop, calls=%fused_computation | loop fusion | bytes 163840 | tf_op jit(solution)/shard_map/slice | solution.py:517

commit v4 on v3

--- a/solution.py
+++ b/solution.py
@@ -71,6 +71,10 @@
     t_next, t_prev = lax.rem(ta + 1, nt), lax.rem(ta + nt - 1, nt)
     z_next, z_prev = lax.rem(sa + 1, nz), lax.rem(sa + nz - 1, nz)
 
+    barrier = pltpu.get_barrier_semaphore()
+    for where_to in ({"ta": t_next}, {"ta": t_prev}, {"sa": z_next}, {"sa": z_prev}):
+        pl.semaphore_signal(barrier, inc=1, device_id=where_to, device_id_type=MESH)
+
     copies = [
         pltpu.make_async_copy(links_ref.at[d], lk.at[d], csem.at[d]) for d in range(4)
     ] + [
@@ -80,10 +84,6 @@
     ]
     for d in (5, 6, 1, 2, 3, 4, 0):
         copies[d].start()
-
-    barrier = pltpu.get_barrier_semaphore()
-    for where_to in ({"ta": t_next}, {"ta": t_prev}, {"sa": z_next}, {"sa": z_prev}):
-        pl.semaphore_signal(barrier, inc=1, device_id=where_to, device_id_type=MESH)
 
     shape = (dof, lanes)
     lane = lax.broadcasted_iota(jnp.int32, shape, 1)

time: 36.5 us -> 36.5 us (level)
  no operation moved by 1% of the time
where the time goes in v4:
time: 36.5 us; the launch traced here: 36.3 us
  Pallas kernels  34.2 us (94%)
  local copies, waits for them, and re-layouts  1.43 us (4%)
  between operations  0.64 us (2%)
    pallas_call x1, Pallas kernels, shards(): pl.pallas_call(functools.partial(kernel, nt, nz), out_shape=jax.ShapeDtyp...  34.2 us
    slice x1, local copies, waits for them, and re-layouts, shards(): return (out[0].reshape(rhs.shape), out[1].reshape(rhs.shape))  1.43 us

profile of v4, /device:TPU:0, one launch (start us, length us, event | category | flops | bytes accessed | tf_op | source)
XLA Modules:
  0.0 36.3 jit_solution(17696704257280423399)
XLA Ops:
  0.6 34.2 %shard_map.59 = f32[2,2,40,128]{3,2,1,0:T(8,128)} custom-call(f32[2,40,128]{2,1,0:T(8,128)} %bitcast.12, bf16[4,2,40,40,128]{4,3,2,1,0:T(8,128)(2,1)} %bitcast.10, bf16[2,40,40,128]{3,2,1,0:T(8,128)(2,1)} %bitcast.11, s32[2]{0:T(128)} %bitcast.15), custom_call_target="tpu_custom_call" | custom-call | tf_op jit(solution)/shard_map/pallas_call | solution.py:474
  34.9 1.4 %fusion = (f32[1,2,40,128]{3,2,1,0:T(8,128)}, f32[1,2,40,128]{3,2,1,0:T(8,128)}) fusion(f32[2,2,40,128]{3,2,1,0:T(8,128)} %shard_map.59), kind=kLoop, calls=%fused_computation | loop fusion | bytes 163840 | tf_op jit(solution)/shard_map/slice | solution.py:517
